TPU v7x, 32 devices: a whole 2x2x4 slice. The times are simulated.
32 devices in a mesh: dp: 32 (over z, y, x, core).
Axes of the slice: x: 2, y: 2, z: 4, core: 2. Of those that a mesh axis runs over, the one named last changes fastest.
Arguments:
- params: float32 [4063232], P('dp'), may hold values from -6 to 6
- first_moment: float32 [4063232], P('dp'), may hold values from -2 to 2
- second_moment: float32 [4063232], P('dp'), may hold values from 0.01 to 1
- grads: bfloat16 [4063232], P('dp'), may hold values from -6 to 6
- old_bounds: int32 [33], replicated, may hold values from 0 to 3932160, as said below
- new_bounds: int32 [33], replicated, may hold values from 0 to 3932160, as said below
- seg_start: int32 [64], replicated, may hold values from 0 to 3932096, as said below
Outputs:
- new_params: float32 [4063232], P('dp')
- new_first: float32 [4063232], P('dp')
- new_second: float32 [4063232], P('dp')
Inputs may be any that keep to these rules, and one draw needn't show every extreme that they name: `old_bounds`: starts at 0 and ends at 3932160; every shard holds between 118784 and 126976 elements, exactly 126976 in some shard. `new_bounds`: starts at 0 and ends at 3932160; every shard holds between 118784 and 126976 elements, exactly 126976 in some shard; each entry differs from the same entry of old_bounds by at most 4096, by exactly 4096 somewhere. `seg_start`: strictly rising, the first is 0, all are multiples of 64.
All inputs are finite; a program needn't handle non-finite values.
Results may differ from a plain program's by a relative error of at most 0.0003.
Values sent between devices are 32-bit elements; how exact they have to be, the bound alone decides.
A program may use at most 64 MiB of HBM per device.

v0:
```python
import jax
import jax.numpy as jnp
from jax import lax
from jax.sharding import PartitionSpec as P

MARGIN = 4096
SEGS = 64


BETA_ONE = 0.9
BETA_TWO = 0.999
CORR_ONE = 1.0 - 0.9**10
CORR_TWO = 1.0 - 0.999**10
DECAY = 0.01
LEARN = 0.1
EPSILON = 1e-06


def shifted(value, axis, steps):
    count = lax.axis_size(axis)
    leading, last = (max(0, -steps), min(count, count - steps))
    return lax.ppermute(value, axis, [(source, source + steps) for source in range(leading, last)])


def shards(params, first_moment, second_moment, grads, old_bounds, new_bounds, seg_start):
    cap = params.shape[0]
    margin = MARGIN
    device = lax.axis_index("dp")
    old_low = old_bounds[device]
    old_count = old_bounds[device + 1] - old_low
    slots = jnp.arange(cap, dtype=jnp.int32)
    live = slots < old_count
    gradient = grads.astype(jnp.float32)
    moment_new = BETA_ONE * first_moment + (1.0 - BETA_ONE) * gradient
    second_new = BETA_TWO * second_moment + (1.0 - BETA_TWO) * gradient * gradient
    update = moment_new / CORR_ONE / (jnp.sqrt(second_new / CORR_TWO) + EPSILON) + DECAY * params
    position = old_low + slots
    segment = jnp.sum((position[:, None] >= seg_start[None, :]).astype(jnp.int32), axis=1) - 1
    labels = jnp.arange(SEGS, dtype=jnp.int32)
    member = (segment[:, None] == labels[None, :]) & live[:, None]
    weight_part = jnp.sum(jnp.where(member, (params * params)[:, None], 0.0), axis=0)
    update_part = jnp.sum(jnp.where(member, (update * update)[:, None], 0.0), axis=0)
    sums = lax.psum(jnp.stack([weight_part, update_part]), "dp")
    ratio = jnp.sqrt(sums[0]) / (jnp.sqrt(sums[1]) + EPSILON)
    element_ratio = jnp.sum(
        jnp.where(segment[:, None] == labels[None, :], ratio[None, :], 0.0), axis=1
    )
    weight_new = params - LEARN * element_ratio * update
    state = jnp.where(live[None, :], jnp.stack([weight_new, moment_new, second_new]), 0.0)
    tail = lax.dynamic_slice_in_dim(state, old_count - margin, margin, 1)
    left_rim = shifted(tail, "dp", 1)
    right_rim = shifted(state[:, :margin], "dp", -1)
    extended = jnp.concatenate([left_rim, state, jnp.zeros((3, margin), jnp.float32)], axis=1)
    extended = lax.dynamic_update_slice_in_dim(extended, right_rim, margin + old_count, 1)
    new_low = new_bounds[device]
    new_count = new_bounds[device + 1] - new_low
    offset = new_low - old_low + margin
    placed = lax.dynamic_slice_in_dim(extended, offset, cap, 1)
    placed = jnp.where((slots < new_count)[None, :], placed, 0.0)
    return (placed[0], placed[1], placed[2])


def solution(mesh):
    placed = (P("dp"), P("dp"), P("dp"), P("dp"), P(), P(), P())
    return jax.shard_map(
        shards, mesh=mesh, in_specs=placed, out_specs=(P("dp"), P("dp"), P("dp")), check_vma=False
    )
```

profile of v0, /device:TPU:8, one launch (start us, length us, event | category | flops | bytes accessed | tf_op | source)
XLA Modules:
  0.0 85.6 jit_solution(1286579094773983819)
XLA Ops:
  0.6 0.0 copy-start.3
  0.6 0.0 copy-start
  0.7 1.5 %fusion.9 = (s32[1]{0:T(128)}, s32[1]{0:T(128)}, s32[1]{0:T(128)}, s32[1]{0:T(128)}) fusion(s32[33]{0:T(128)} %param.12, s32[]{:T(128)S(6)} %select_n.35, s32[]{:T(128)S(6)} %select_n.36, s32[33]{0:T(128)} %param.11), kind=kLoop, calls=%fused_computation.26 | loop fusion | bytes 40 | tf_op jit(solution)/shard_map/dynamic_slice | solution.py:56
  2.1 0.7 iota_add_fusion
  4.1 0.0 copy-start.1
  4.1 0.0 copy-start.2
  4.2 0.1 iota_compare_fusion.1
  4.2 4.7 %convert_reduce_fusion = s32[126976]{0:T(1024)S(1)} fusion(s32[126976]{0:T(1024)S(1)} %iota_add_fusion, s32[64]{0:T(128)} %param.13), kind=kLoop, calls=%fused_computation.5 | loop fusion | flops 24252416 | bytes 1016064 | tf_op jit(solution)/shard_map/reduce_sum | solution.py:38
  9.1 0.4 fusion.4
  9.5 9.1 %select_reduce_fusion.2 = (f32[64]{0:T(128)S(1)}, f32[64]{0:T(128)S(1)}) fusion(f32[126976]{0:T(1024)S(1)} %get-tuple-element.13, s32[126976]{0:T(1024)S(1)} %broadcast_add_fusion, pred[126976]{0:T(1024)(128)(4,1)S(1)} %iota_compare_fusion.1, f32[126976]{0:T(1024)S(1)} %get-tuple-element.5), kind=kLoop, calls=%fused_computation.2 | loop fusion | flops 48758656 | bytes 1651200 | tf_op jit(solution)/shard_map/reduce_sum | solution.py:41
  18.7 40.6 %psum.7 = f32[2,64]{1,0:T(2,128)S(1)} all-reduce(f32[2,64]{1,0:T(2,128)S(1)} %pad_maximum_fusion), channel_id=1, replica_groups=mesh['dp'=32] {'dp'}, use_global_device_ids=true, to_apply=%region_3.4 | all-reduce | flops 128 | bytes 1024 | tf_op jit(solution)/shard_map/psum | solution.py:43
  59.3 5.1 %select_reduce_fusion = f32[126976]{0:T(1024)S(1)} fusion(f32[64]{0:T(128)S(1)} %fusion.3, s32[126976]{0:T(1024)S(1)} %broadcast_add_fusion), kind=kLoop, calls=%fused_computation | loop fusion | flops 24252416 | bytes 1016064 | tf_op jit(solution)/shard_map/reduce_sum | solution.py:45
  64.4 0.3 multiply_subtract_fusion
  64.7 1.8 %maximum_select_fusion = f32[3,126976]{1,0:T(4,128)S(1)} fusion(f32[1,126976]{1,0:T(1,128)S(1)} %bitcast.15, f32[1,126976]{1,0:T(1,128)S(1)} %bitcast.14, f32[1,126976]{1,0:T(1,128)S(1)} %bitcast.16, pred[126976]{0:T(1024)(128)(4,1)S(1)} %iota_compare_fusion.1), kind=kLoop, calls=%fused_computation.7 | loop fusion | flops 1142784 | bytes 3174400 | tf_op jit(solution)/shard_map/jit(_where)/select_n | solution.py:49
  66.5 0.1 fusion.8
  66.6 1.9 %collective-permute-start = (f32[3,4096]{1,0:T(4,128)S(1)}, f32[3,4096]{1,0:T(4,128)S(1)}, u32[]{:S(2)}, u32[]{:S(2)}) collective-permute-start(f32[3,4096]{1,0:T(4,128)S(1)} %get-tuple-element.12), channel_id=1, source_target_pairs={{0,1},{1,2},{2,3},{3,4},{4,5},{5,6},{6,7},{7,8},{8,9},{9,10},{10,1... | collective-permute-start | bytes 147464 | tf_op jit(solution)/shard_map/ppermute | solution.py:22
  68.5 5.4 %collective-permute-start.1 = (f32[3,4096]{1,0:T(4,128)S(1)}, f32[3,4096]{1,0:T(4,128)S(1)}, u32[]{:S(2)}, u32[]{:S(2)}) collective-permute-start(f32[3,4096]{1,0:T(4,128)S(1)} %get-tuple-element.11), channel_id=1, source_target_pairs={{1,0},{2,1},{3,2},{4,3},{5,4},{6,5},{7,6},{8,7},{9,8},{10,9},{11,1... | collective-permute-start | bytes 147464 | tf_op jit(solution)/shard_map/ppermute | solution.py:22
  75.3 0.1 iota_compare_fusion.2
  76.8 0.0 collective-permute-done
  76.8 2.0 %maximum_maximum_fusion = f32[3,135168]{1,0:T(4,128)} fusion(f32[3,126976]{1,0:T(4,128)S(1)} %maximum_select_fusion, f32[3,4096]{1,0:T(4,128)S(1)} %collective-permute-done, f32[135168]{0:T(1024)S(1)} %pad.2.clone), kind=kLoop, calls=%fused_computation.6 | loop fusion | flops 811008 | bytes 3735552 | tf_op jit(solution)/shard_map/concatenate | solution.py:53
  78.8 0.0 collective-permute-done.1
  78.8 1.8 %dynamic_update_slice.3 = f32[3,135168]{1,0:T(4,128)} dynamic-update-slice(f32[3,135168]{1,0:T(4,128)} %maximum_maximum_fusion, f32[3,4096]{1,0:T(4,128)S(1)} %collective-permute-done.1, s32[]{:T(128)} %constant.10.clone.1, s32[]{:T(128)S(6)} %select_n.42) | dynamic-update-slice | bytes 98308 | tf_op jit(solution)/shard_map/dynamic_update_slice | solution.py:54
  80.6 2.7 %dynamic-slice_select_fusion = f32[3,126976]{1,0:T(4,128)S(1)} fusion(f32[3,135168]{1,0:T(4,128)} %dynamic_update_slice.3, s32[]{:T(128)S(6)} %select_n.43, pred[126976]{0:T(1024)(128)(4,1)S(1)} %iota_compare_fusion.2), kind=kLoop, calls=%fused_computation.8 | loop fusion | flops 380928 | bytes 3174404 | tf_op jit(solution)/shard_map/jit(_where)/select_n | solution.py:59
  83.3 2.3 %fusion.7 = (f32[1,126976]{1,0:T(1,128)}, f32[1,126976]{1,0:T(1,128)}, f32[1,126976]{1,0:T(1,128)}) fusion(f32[3,126976]{1,0:T(4,128)S(1)} %dynamic-slice_select_fusion), kind=kLoop, calls=%fused_computation.24 | loop fusion | bytes 3047424 | tf_op jit(solution)/shard_map/slice | solution.py:60
  (9 shorter events, 0.1 us)
Async XLA Ops:
  0.6 8.4 %copy-start.3 = (bf16[126976]{0:T(1024)(128)(2,1)S(1)}, bf16[126976]{0:T(1024)(128)(2,1)}, u32[]{:S(2)}) copy-start(bf16[126976]{0:T(1024)(128)(2,1)} %param.10) | copy-start | bytes 761860
  0.6 8.4 %copy-start = (f32[126976]{0:T(1024)S(1)}, f32[126976]{0:T(1024)}, u32[]{:S(2)}) copy-start(f32[126976]{0:T(1024)} %param.7) | copy-start | bytes 1523716
  4.1 4.9 %copy-start.1 = (f32[126976]{0:T(1024)S(1)}, f32[126976]{0:T(1024)}, u32[]{:S(2)}) copy-start(f32[126976]{0:T(1024)} %param.8) | copy-start | bytes 1523716
  4.1 4.9 %copy-start.2 = (f32[126976]{0:T(1024)S(1)}, f32[126976]{0:T(1024)}, u32[]{:S(2)}) copy-start(f32[126976]{0:T(1024)} %param.9) | copy-start | bytes 1523716
  66.6 10.1 %collective-permute-start = (f32[3,4096]{1,0:T(4,128)S(1)}, f32[3,4096]{1,0:T(4,128)S(1)}, u32[]{:S(2)}, u32[]{:S(2)}) collective-permute-start(f32[3,4096]{1,0:T(4,128)S(1)} %get-tuple-element.12), channel_id=1, source_target_pairs={{0,1},{1,2},{2,3},{3,4},{4,5},{5,6},{6,7},{7,8},{8,9},{9,10},{10,1... | collective-permute-start | bytes 147464 | tf_op jit(solution)/shard_map/ppermute | solution.py:22
  68.5 10.2 %collective-permute-start.1 = (f32[3,4096]{1,0:T(4,128)S(1)}, f32[3,4096]{1,0:T(4,128)S(1)}, u32[]{:S(2)}, u32[]{:S(2)}) collective-permute-start(f32[3,4096]{1,0:T(4,128)S(1)} %get-tuple-element.11), channel_id=1, source_target_pairs={{1,0},{2,1},{3,2},{4,3},{5,4},{6,5},{7,6},{8,7},{9,8},{10,9},{11,1... | collective-permute-start | bytes 147464 | tf_op jit(solution)/shard_map/ppermute | solution.py:22
where the time goes:
time: 86 us; the launch traced here: 85.6 us
  blocking collectives  40.6 us (47%)
  other arithmetic  27.1 us (32%)
  starting transfers between devices  7.36 us (9%)
  local copies, waits for them, and re-layouts  5.71 us (7%)
  between operations  4.78 us (6%)
    psum x1, blocking collectives, shards(): sums = lax.psum(jnp.stack([weight_part, update_part]), 'dp')  40.6 us
    reduce_sum x1, other arithmetic, shards(): jnp.sum(jnp.where(member, (params * params)[:, None], 0.0), axis=0)  9.14 us
    ppermute x2, starting transfers between devices, shifted(): lax.ppermute(value, axis, [(source, source + steps) for source in range(l...  7.36 us
    reduce_sum x1, other arithmetic, shards(): jnp.sum(jnp.where(segment[:, None] == labels[None, :], ratio[None, :], 0....  5.1 us
    reduce_sum x1, other arithmetic, shards(): jnp.sum((position[:, None] >= seg_start[None, :]).astype(jnp.int32), axis=1)  4.75 us
    select_n x1, other arithmetic, shards(): placed = jnp.where((slots < new_count)[None, :], placed, 0.0)  2.68 us
    slice x1, local copies, waits for them, and re-layouts, shards(): return (placed[0], placed[1], placed[2])  2.26 us
    concatenate x1, other arithmetic, shards(): jnp.concatenate([left_rim, state, jnp.zeros((3, margin), jnp.float32)], a...  2.01 us
  transfers between devices with their start and end apart: 2, of which 0 were waited for; matrix products, arithmetic and copies ran while one was open for 2% of the time, Pallas kernels for 0%

commit v1 on v0

v1 whole, which is shorter than its diff:
```python
import functools

import jax
import jax.numpy as jnp
from jax import lax
from jax.experimental import pallas as pl
from jax.experimental.pallas import tpu as pltpu
from jax.sharding import PartitionSpec as P

MARGIN = 4096
LANES = 128
BLOCK = MARGIN // LANES
PAD = BLOCK + 8
EDGE = 2 * PAD + BLOCK


BETA_ONE = 0.9
BETA_TWO = 0.999
CORR_ONE = 1.0 - 0.9**10
CORR_TWO = 1.0 - 0.999**10
DECAY = 0.01
LEARN = 0.1
EPSILON = 1e-06

MESH = pl.DeviceIdType.MESH
VMEM_LIMIT = 16 * 1024 * 1024


def lane_ids(rows=BLOCK):
    return lax.broadcasted_iota(jnp.int32, (rows, LANES), 1)


def flat_ids():
    return lax.broadcasted_iota(jnp.int32, (BLOCK, LANES), 0) * LANES + lane_ids()


def moved(first, second, lanes):
    picked = jnp.where(lane_ids() >= lanes, first, second)
    return pltpu.roll(picked, (LANES - lanes) & (LANES - 1), 1)


def overlapping(seg_ref, low, high):
    def step(s, carry):
        first, end = carry
        start = seg_ref[s]
        return (first + (start <= low).astype(jnp.int32), end + (start < high).astype(jnp.int32))

    first, end = lax.fori_loop(0, seg_ref.shape[0], step, (jnp.int32(-1), jnp.int32(0)), unroll=8)
    return first, end


def span_of(seg_ref, s, low, count):
    segs = seg_ref.shape[0]
    begin = jnp.maximum(seg_ref[s] - low, 0)
    after = seg_ref[jnp.minimum(s + 1, segs - 1)] - low
    finish = jnp.where(s + 1 < segs, jnp.minimum(after, count), count)
    return begin, finish


def update_kernel(axis, old_ref, seg_ref, w_hbm, m_hbm, v_hbm, g_hbm, state, part, tail, head, m_buf, v_buf, g_buf, sems):
    rows = m_buf.shape[0]
    blocks = rows // BLOCK
    step_blocks = -(-blocks // sems.shape[1])
    chunks = [(b, min(b + step_blocks, blocks)) for b in range(0, blocks, step_blocks)]
    copies = []
    for c, (b0, b1) in enumerate(chunks):
        window = pl.ds(b0 * BLOCK, (b1 - b0) * BLOCK)
        placed = state.at[0, pl.ds(PAD + b0 * BLOCK, (b1 - b0) * BLOCK)]
        group = [
            pltpu.make_async_copy(w_hbm.at[window], placed, sems.at[0, c]),
            pltpu.make_async_copy(m_hbm.at[window], m_buf.at[window], sems.at[1, c]),
            pltpu.make_async_copy(v_hbm.at[window], v_buf.at[window], sems.at[2, c]),
            pltpu.make_async_copy(g_hbm.at[window], g_buf.at[window], sems.at[3, c]),
        ]
        for copy in group:
            copy.start()
        copies.append(group)

    me = lax.axis_index(axis)
    low = old_ref[me]
    high = old_ref[me + 1]
    count = high - low
    first, end = overlapping(seg_ref, low, high)

    def advance(b, carry):
        here = pl.multiple_of(b * BLOCK, BLOCK)
        there = pl.multiple_of(b * BLOCK + PAD, 8)
        gradient = g_buf[pl.ds(here, BLOCK), :].astype(jnp.float32)
        weight = state[0, pl.ds(there, BLOCK), :]
        moment = BETA_ONE * m_buf[pl.ds(here, BLOCK), :] + (1.0 - BETA_ONE) * gradient
        second = BETA_TWO * v_buf[pl.ds(here, BLOCK), :] + (1.0 - BETA_TWO) * gradient * gradient
        scaled = moment * (1.0 / CORR_ONE)
        update = scaled / (jnp.sqrt(second * (1.0 / CORR_TWO)) + EPSILON) + DECAY * weight
        state[1, pl.ds(there, BLOCK), :] = update
        state[2, pl.ds(there, BLOCK), :] = moment
        state[3, pl.ds(there, BLOCK), :] = second
        return carry

    for (b0, b1), group in zip(chunks, copies):
        for copy in group:
            copy.wait()
        lax.fori_loop(b0, b1, advance, 0)

    flat = flat_ids()
    lane = lane_ids(1)
    segs = seg_ref.shape[0]

    def tensor(s, row):
        begin, finish = span_of(seg_ref, s, low, count)

        def add(b, carry):
            there = pl.multiple_of(b * BLOCK + PAD, 8)
            index = flat + b * MARGIN
            inside = (index >= begin) & (index < finish)
            weight = state[0, pl.ds(there, BLOCK), :]
            update = state[1, pl.ds(there, BLOCK), :]
            return (
                carry[0] + jnp.where(inside, weight * weight, 0.0),
                carry[1] + jnp.where(inside, update * update, 0.0),
            )

        nothing = jnp.zeros((BLOCK, LANES), jnp.float32)
        weights, updates = lax.fori_loop(
            begin // MARGIN, (finish + MARGIN - 1) // MARGIN, add, (nothing, nothing)
        )
        row = jnp.where(lane == s, jnp.sum(weights, axis=(0, 1), keepdims=True), row)
        return jnp.where(lane == s + segs, jnp.sum(updates, axis=(0, 1), keepdims=True), row)

    part[...] = lax.fori_loop(first, end, tensor, jnp.zeros((1, LANES), jnp.float32))

    start = count - MARGIN
    top = start // LANES
    lanes = start & (LANES - 1)
    for a in range(4):
        head[a] = state[a, PAD : PAD + BLOCK, :]
        tail[a] = moved(
            state[a, pl.ds(PAD + top, BLOCK), :], state[a, pl.ds(PAD + top + 1, BLOCK), :], lanes
        )


def exchange_kernel(axis, n, part, tail, head, sums, left_rim, right_rim, slots, send, receive, rim_send, rim_receive):
    me = lax.axis_index(axis)
    right = lax.rem(me + 1, n)
    left = lax.rem(me + n - 1, n)
    barrier = pltpu.get_barrier_semaphore()

    def greet(k, carry):
        pl.semaphore_signal(barrier, inc=1, device_id=(lax.rem(me + k, n),), device_id_type=MESH)
        return carry

    lax.fori_loop(1, n, greet, 0)
    slots[me] = part[...]
    pl.semaphore_wait(barrier, n - 1)

    def tell(k):
        return pltpu.make_async_remote_copy(
            src_ref=part,
            dst_ref=slots.at[me],
            send_sem=send.at[k],
            recv_sem=receive.at[k],
            device_id=(lax.rem(me + k, n),),
            device_id_type=MESH,
        )

    def hear(k):
        source = lax.rem(me + n - k, n)
        return pltpu.make_async_remote_copy(
            src_ref=part,
            dst_ref=slots.at[source],
            send_sem=send.at[k],
            recv_sem=receive.at[k],
            device_id=(source,),
            device_id_type=MESH,
        )

    onward = pltpu.make_async_remote_copy(
        src_ref=tail,
        dst_ref=left_rim,
        send_sem=rim_send.at[0],
        recv_sem=rim_receive.at[0],
        device_id=(right,),
        device_id_type=MESH,
    )
    back = pltpu.make_async_remote_copy(
        src_ref=head,
        dst_ref=right_rim,
        send_sem=rim_send.at[1],
        recv_sem=rim_receive.at[1],
        device_id=(left,),
        device_id_type=MESH,
    )

    def start(k, carry):
        tell(k).start()
        return carry

    def finish(k, carry):
        tell(k).wait_send()
        hear(k).wait_recv()
        return carry

    lax.fori_loop(1, n, start, 0)
    onward.start()
    back.start()
    lax.fori_loop(1, n, finish, 0)
    sums[...] = jnp.sum(slots[...], axis=0)
    onward.wait()
    back.wait()


def place_kernel(axis, old_ref, new_ref, seg_ref, state, sums, left_rim, right_rim, w_out, m_out, v_out, w_buf, u_buf, m_buf, v_buf, before, after, sems):
    rows = w_buf.shape[0]
    blocks = rows // BLOCK
    me = lax.axis_index(axis)
    old_low = old_ref[me]
    old_count = old_ref[me + 1] - old_low
    new_low = new_ref[me]
    new_high = new_ref[me + 1]
    new_count = new_high - new_low
    shift = new_low - old_low
    top = shift // LANES
    lanes = shift & (LANES - 1)
    flat = flat_ids()
    targets = (w_buf, u_buf, m_buf, v_buf)

    for a in range(4):
        before[a, 0:BLOCK, :] = left_rim[a]
        before[a, BLOCK:EDGE, :] = state[a, PAD : PAD + EDGE - BLOCK, :]
        after[a, PAD : PAD + BLOCK, :] = right_rim[a]
        targets[a][0:BLOCK, :] = moved(
            before[a, pl.ds(BLOCK + top, BLOCK), :], before[a, pl.ds(BLOCK + top + 1, BLOCK), :], lanes
        )

    def own(a, b):
        there = b * BLOCK + PAD + top
        return moved(state[a, pl.ds(there, BLOCK), :], state[a, pl.ds(there + 1, BLOCK), :], lanes)

    def inner(b, carry):
        here = pl.multiple_of(b * BLOCK, BLOCK)
        for a in range(4):
            targets[a][pl.ds(here, BLOCK), :] = own(a, b)
        return carry

    lax.fori_loop(1, blocks - 3, inner, 0)

    for b in range(blocks - 3, blocks):
        offset = b * MARGIN + shift - old_count
        row = jnp.clip(offset // LANES, -PAD, PAD - 7) + PAD
        side = offset & (LANES - 1)
        index = flat + b * MARGIN
        beyond = index + shift >= old_count
        live = index < new_count
        for a in range(4):
            rim = moved(after[a, pl.ds(row, BLOCK), :], after[a, pl.ds(row + 1, BLOCK), :], side)
            value = jnp.where(beyond, rim, own(a, b))
            targets[a][b * BLOCK : (b + 1) * BLOCK, :] = jnp.where(live, value, 0.0)

    m_copy = pltpu.make_async_copy(m_buf, m_out, sems.at[1])
    v_copy = pltpu.make_async_copy(v_buf, v_out, sems.at[2])
    m_copy.start()
    v_copy.start()

    segs = seg_ref.shape[0]
    total = sums[...]
    other = pltpu.roll(total, LANES - segs, 1)
    rate = LEARN * (jnp.sqrt(total) / (jnp.sqrt(other) + EPSILON))
    lane = lane_ids(1)
    first, end = overlapping(seg_ref, new_low, new_high)

    def tensor(s, carry):
        begin, finish = span_of(seg_ref, s, new_low, new_count)
        factor = jnp.sum(jnp.where(lane == s, rate, 0.0), axis=1, keepdims=True)

        def apply(b, inner_carry):
            here = pl.ds(pl.multiple_of(b * BLOCK, BLOCK), BLOCK)
            index = flat + b * MARGIN
            inside = (index >= begin) & (index < finish)
            weight = w_buf[here, :]
            w_buf[here, :] = jnp.where(inside, weight - factor * u_buf[here, :], weight)
            return inner_carry

        return lax.fori_loop(begin // MARGIN, (finish + MARGIN - 1) // MARGIN, apply, carry)

    lax.fori_loop(first, end, tensor, 0)
    w_copy = pltpu.make_async_copy(w_buf, w_out, sems.at[0])
    w_copy.start()
    m_copy.wait()
    v_copy.wait()
    w_copy.wait()


def spec(space):
    return pl.BlockSpec(memory_space=space)


def shards(axis, n, params, first_moment, second_moment, grads, old_bounds, new_bounds, seg_start):
    cap = params.shape[0]
    rows = cap // LANES
    f32 = jnp.float32
    flat = [x.reshape(rows, LANES) for x in (params, first_moment, second_moment, grads)]
    rim = jax.ShapeDtypeStruct((4, BLOCK, LANES), f32)
    line = jax.ShapeDtypeStruct((1, LANES), f32)
    smem, vmem, hbm = spec(pltpu.SMEM), spec(pltpu.VMEM), spec(pl.ANY)
    state, part, tail, head = pl.pallas_call(
        functools.partial(update_kernel, axis),
        name="update",
        out_shape=(jax.ShapeDtypeStruct((4, rows + 2 * PAD, LANES), f32), line, rim, rim),
        in_specs=[smem, smem, hbm, hbm, hbm, hbm],
        out_specs=(vmem,) * 4,
        scratch_shapes=[
            pltpu.VMEM((rows, LANES), f32),
            pltpu.VMEM((rows, LANES), f32),
            pltpu.VMEM((rows, LANES), grads.dtype),
            pltpu.SemaphoreType.DMA((4, 4)),
        ],
        compiler_params=pltpu.CompilerParams(vmem_limit_bytes=VMEM_LIMIT),
    )(old_bounds, seg_start, *flat)
    sums, left_rim, right_rim = pl.pallas_call(
        functools.partial(exchange_kernel, axis, n),
        name="exchange",
        out_shape=(line, rim, rim),
        in_specs=[vmem] * 3,
        out_specs=(vmem,) * 3,
        scratch_shapes=[
            pltpu.VMEM((n, 1, LANES), f32),
            pltpu.SemaphoreType.DMA((n,)),
            pltpu.SemaphoreType.DMA((n,)),
            pltpu.SemaphoreType.DMA((2,)),
            pltpu.SemaphoreType.DMA((2,)),
        ],
        compiler_params=pltpu.CompilerParams(
            collective_id=0, has_side_effects=True, vmem_limit_bytes=VMEM_LIMIT
        ),
    )(part, tail, head)
    whole = jax.ShapeDtypeStruct((rows, LANES), f32)
    outs = pl.pallas_call(
        functools.partial(place_kernel, axis),
        name="place",
        out_shape=(whole,) * 3,
        in_specs=[smem, smem, smem, vmem, vmem, vmem, vmem],
        out_specs=(hbm,) * 3,
        scratch_shapes=[pltpu.VMEM((rows, LANES), f32)] * 4
        + [pltpu.VMEM((4, EDGE, LANES), f32)] * 2
        + [pltpu.SemaphoreType.DMA((3,))],
        compiler_params=pltpu.CompilerParams(vmem_limit_bytes=VMEM_LIMIT),
    )(old_bounds, new_bounds, seg_start, state, sums, left_rim, right_rim)
    return tuple(x.reshape(cap) for x in outs)


def solution(mesh):
    (axis,) = mesh.axis_names
    n = mesh.shape[axis]
    placed = (P(axis), P(axis), P(axis), P(axis), P(), P(), P())
    return jax.shard_map(
        functools.partial(shards, axis, n),
        mesh=mesh,
        in_specs=placed,
        out_specs=(P(axis), P(axis), P(axis)),
        check_vma=False,
    )
```

time: 86 us -> 27.6 us (0.32)
  the two profiles are of different devices: /device:TPU:8 before, /device:TPU:0 now
where the time goes in v1:
time: 27.6 us; the launch traced here: 27.3 us
  Pallas kernels  20 us (72%)
  local copies, waits for them, and re-layouts  6.66 us (24%)
  between operations  0.67 us (2%)
    pallas_call x1, Pallas kernels, shards(): pl.pallas_call(functools.partial(exchange_kernel, axis, n), name='exchang...  10.7 us
    unnamed x16, local copies, waits for them, and re-layouts  6.66 us
    pallas_call x1, Pallas kernels, shards(): pl.pallas_call(functools.partial(update_kernel, axis), name='update', out...  4.76 us
    pallas_call x1, Pallas kernels, shards(): pl.pallas_call(functools.partial(place_kernel, axis), name='place', out_s...  4.54 us

profile of v1, /device:TPU:0, one launch (start us, length us, event | category | flops | bytes accessed | tf_op | source)
XLA Modules:
  0.0 27.3 jit_solution(14191907662927652789)
XLA Ops:
  0.6 0.0 copy-start
  0.6 1.0 %copy-done = f32[126976]{0:T(1024)S(1)} copy-done((f32[126976]{0:T(1024)S(1)}, f32[126976]{0:T(1024)}, u32[]{:S(2)}) %copy-start) | copy-done | bytes 507928
  1.7 0.0 copy-start.1
  1.7 1.0 %copy-done.1 = f32[126976]{0:T(1024)S(1)} copy-done((f32[126976]{0:T(1024)S(1)}, f32[126976]{0:T(1024)}, u32[]{:S(2)}) %copy-start.1) | copy-done | bytes 507928
  2.7 0.0 copy-start.2
  2.7 1.0 %copy-done.2 = f32[126976]{0:T(1024)S(1)} copy-done((f32[126976]{0:T(1024)S(1)}, f32[126976]{0:T(1024)}, u32[]{:S(2)}) %copy-start.2) | copy-done | bytes 507928
  3.7 0.0 copy-start.3
  3.7 0.9 %copy-done.3 = bf16[126976]{0:T(1024)(128)(2,1)S(1)} copy-done((bf16[126976]{0:T(1024)(128)(2,1)S(1)}, bf16[126976]{0:T(1024)(128)(2,1)}, u32[]{:S(2)}) %copy-start.3) | copy-done | bytes 253976
  4.7 0.0 copy-start.4
  4.7 0.7 %copy-done.4 = s32[33]{0:T(128)S(1)} copy-done((s32[33]{0:T(128)S(1)}, s32[33]{0:T(128)}, u32[]{:S(2)}) %copy-start.4) | copy-done | bytes 156
  5.3 0.0 copy-start.6
  5.3 0.7 %copy-done.6 = s32[64]{0:T(128)S(1)} copy-done((s32[64]{0:T(128)S(1)}, s32[64]{0:T(128)}, u32[]{:S(2)}) %copy-start.6) | copy-done | bytes 280
  6.0 4.8 %update.1 = (f32[4,1072,128]{2,1,0:T(8,128)S(1)}, f32[1,128]{1,0:T(1,128)S(1)}, f32[4,32,128]{2,1,0:T(8,128)S(1)}, f32[4,32,128]{2,1,0:T(8,128)S(1)}) custom-call(s32[33]{0:T(128)S(1)} %copy-done.4, s32[64]{0:T(128)S(1)} %copy-done.6, f32[992,128]{1,0:T(8,128)S(1)} %bitcast.7, f32[992,128]{1,0:T(8,128)S(1)} %bitcast.8, f32[992,128]{1,0:T(8,128)S(1)} %bitcast.9, ...), custom_call_target="tpu_custom_call" | custom-call | tf_op jit(solution)/shard_map/update/pallas_call | solution.py:304
  10.8 10.7 %exchange.1 = (f32[1,128]{1,0:T(1,128)S(1)}, f32[4,32,128]{2,1,0:T(8,128)S(1)}, f32[4,32,128]{2,1,0:T(8,128)S(1)}) custom-call(f32[1,128]{1,0:T(1,128)S(1)} %get-tuple-element.14.part, f32[4,32,128]{2,1,0:T(8,128)S(1)} %get-tuple-element.15.tail, f32[4,32,128]{2,1,0:T(8,128)S(1)} %get-tuple-element.16.head), custom_call_target="tpu_custom_call" | custom-call | tf_op jit(solution)/shard_map/exchange/pallas_call | solution.py:318
  21.4 0.0 copy-start.5
  21.5 0.6 %copy-done.5 = s32[33]{0:T(128)S(1)} copy-done((s32[33]{0:T(128)S(1)}, s32[33]{0:T(128)}, u32[]{:S(2)}) %copy-start.5) | copy-done | bytes 156
  22.1 0.0 copy-start.7
  22.1 0.7 %copy-done.7 = s32[33]{0:T(128)S(1)} copy-done((s32[33]{0:T(128)S(1)}, s32[33]{0:T(128)}, u32[]{:S(2)}) %copy-start.7) | copy-done | bytes 156
  22.8 4.5 %place.1 = (f32[992,128]{1,0:T(8,128)}, f32[992,128]{1,0:T(8,128)}, f32[992,128]{1,0:T(8,128)}) custom-call(s32[33]{0:T(128)S(1)} %copy-done.5, s32[33]{0:T(128)S(1)} %copy-done.7, s32[64]{0:T(128)S(1)} %copy-done.6, f32[4,1072,128]{2,1,0:T(8,128)S(1)} %get-tuple-element.13.state, f32[1,128]{1,0:T(1,128)S(1)} %get-tuple-element.17.sums, ...), custom_call_target="tpu_custom_call" | custom-call | tf_op jit(solution)/shard_map/place/pallas_call | solution.py:336
Async XLA Ops:
  0.6 1.0 %copy-start = (f32[126976]{0:T(1024)S(1)}, f32[126976]{0:T(1024)}, u32[]{:S(2)}) copy-start(f32[126976]{0:T(1024)} %param.7) | copy-start | bytes 1523716
  1.7 1.0 %copy-start.1 = (f32[126976]{0:T(1024)S(1)}, f32[126976]{0:T(1024)}, u32[]{:S(2)}) copy-start(f32[126976]{0:T(1024)} %param.8) | copy-start | bytes 1523716
  2.7 1.0 %copy-start.2 = (f32[126976]{0:T(1024)S(1)}, f32[126976]{0:T(1024)}, u32[]{:S(2)}) copy-start(f32[126976]{0:T(1024)} %param.9) | copy-start | bytes 1523716
  3.7 0.9 %copy-start.3 = (bf16[126976]{0:T(1024)(128)(2,1)S(1)}, bf16[126976]{0:T(1024)(128)(2,1)}, u32[]{:S(2)}) copy-start(bf16[126976]{0:T(1024)(128)(2,1)} %param.10) | copy-start | bytes 761860
  4.7 0.7 %copy-start.4 = (s32[33]{0:T(128)S(1)}, s32[33]{0:T(128)}, u32[]{:S(2)}) copy-start(s32[33]{0:T(128)} %old_ref.3) | copy-start | bytes 400
  5.3 0.7 %copy-start.6 = (s32[64]{0:T(128)S(1)}, s32[64]{0:T(128)}, u32[]{:S(2)}) copy-start(s32[64]{0:T(128)} %seg_ref.3) | copy-start | bytes 772
  21.4 0.7 %copy-start.5 = (s32[33]{0:T(128)S(1)}, s32[33]{0:T(128)}, u32[]{:S(2)}) copy-start(s32[33]{0:T(128)} %old_ref.3) | copy-start | bytes 400
  22.1 0.7 %copy-start.7 = (s32[33]{0:T(128)S(1)}, s32[33]{0:T(128)}, u32[]{:S(2)}) copy-start(s32[33]{0:T(128)} %new_ref.1) | copy-start | bytes 400

commit v2 on v1

--- a/solution.py
+++ b/solution.py
@@ -57,8 +57,16 @@
     return begin, finish
 
 
-def update_kernel(axis, old_ref, seg_ref, w_hbm, m_hbm, v_hbm, g_hbm, state, part, tail, head, m_buf, v_buf, g_buf, sems):
+def fetched(tables, refs, sems):
+    copies = [pltpu.make_async_copy(t, r, sems.at[i]) for i, (t, r) in enumerate(zip(tables, refs))]
+    for copy in copies:
+        copy.start()
+    return copies
+
+
+def update_kernel(axis, old_hbm, seg_hbm, w_hbm, m_hbm, v_hbm, g_hbm, state, part, tail, head, m_buf, v_buf, g_buf, old_ref, seg_ref, sems, table_sems):
     rows = m_buf.shape[0]
+    tables = fetched((old_hbm, seg_hbm), (old_ref, seg_ref), table_sems)
     blocks = rows // BLOCK
     step_blocks = -(-blocks // sems.shape[1])
     chunks = [(b, min(b + step_blocks, blocks)) for b in range(0, blocks, step_blocks)]
@@ -76,6 +84,8 @@
             copy.start()
         copies.append(group)
 
+    for copy in tables:
+        copy.wait()
     me = lax.axis_index(axis)
     low = old_ref[me]
     high = old_ref[me + 1]
@@ -208,9 +218,16 @@
     back.wait()
 
 
-def place_kernel(axis, old_ref, new_ref, seg_ref, state, sums, left_rim, right_rim, w_out, m_out, v_out, w_buf, u_buf, m_buf, v_buf, before, after, sems):
+def place_kernel(axis, old_hbm, new_hbm, seg_hbm, state, sums, left_rim, right_rim, w_out, m_out, v_out, w_buf, u_buf, m_buf, v_buf, before, after, old_ref, new_ref, seg_ref, sems, table_sems):
+    tables = fetched((old_hbm, new_hbm, seg_hbm), (old_ref, new_ref, seg_ref), table_sems)
     rows = w_buf.shape[0]
     blocks = rows // BLOCK
+    for a in range(4):
+        before[a, 0:BLOCK, :] = left_rim[a]
+        before[a, BLOCK:EDGE, :] = state[a, PAD : PAD + EDGE - BLOCK, :]
+        after[a, PAD : PAD + BLOCK, :] = right_rim[a]
+    for copy in tables:
+        copy.wait()
     me = lax.axis_index(axis)
     old_low = old_ref[me]
     old_count = old_ref[me + 1] - old_low
@@ -224,9 +241,6 @@
     targets = (w_buf, u_buf, m_buf, v_buf)
 
     for a in range(4):
-        before[a, 0:BLOCK, :] = left_rim[a]
-        before[a, BLOCK:EDGE, :] = state[a, PAD : PAD + EDGE - BLOCK, :]
-        after[a, PAD : PAD + BLOCK, :] = right_rim[a]
         targets[a][0:BLOCK, :] = moved(
             before[a, pl.ds(BLOCK + top, BLOCK), :], before[a, pl.ds(BLOCK + top + 1, BLOCK), :], lanes
         )
@@ -298,20 +312,28 @@
     rows = cap // LANES
     f32 = jnp.float32
     flat = [x.reshape(rows, LANES) for x in (params, first_moment, second_moment, grads)]
+    old_bounds, new_bounds, seg_start, *flat = (
+        pltpu.with_memory_space_constraint(x, pltpu.HBM) for x in (old_bounds, new_bounds, seg_start, *flat)
+    )
     rim = jax.ShapeDtypeStruct((4, BLOCK, LANES), f32)
     line = jax.ShapeDtypeStruct((1, LANES), f32)
-    smem, vmem, hbm = spec(pltpu.SMEM), spec(pltpu.VMEM), spec(pl.ANY)
+    vmem, hbm = spec(pltpu.VMEM), spec(pltpu.HBM)
+    bounds = pltpu.SMEM(old_bounds.shape, jnp.int32)
+    starts = pltpu.SMEM(seg_start.shape, jnp.int32)
     state, part, tail, head = pl.pallas_call(
         functools.partial(update_kernel, axis),
         name="update",
         out_shape=(jax.ShapeDtypeStruct((4, rows + 2 * PAD, LANES), f32), line, rim, rim),
-        in_specs=[smem, smem, hbm, hbm, hbm, hbm],
+        in_specs=[hbm] * 6,
         out_specs=(vmem,) * 4,
         scratch_shapes=[
             pltpu.VMEM((rows, LANES), f32),
             pltpu.VMEM((rows, LANES), f32),
             pltpu.VMEM((rows, LANES), grads.dtype),
+            bounds,
+            starts,
             pltpu.SemaphoreType.DMA((4, 4)),
+            pltpu.SemaphoreType.DMA((2,)),
         ],
         compiler_params=pltpu.CompilerParams(vmem_limit_bytes=VMEM_LIMIT),
     )(old_bounds, seg_start, *flat)
@@ -337,11 +359,11 @@
         functools.partial(place_kernel, axis),
         name="place",
         out_shape=(whole,) * 3,
-        in_specs=[smem, smem, smem, vmem, vmem, vmem, vmem],
+        in_specs=[hbm, hbm, hbm, vmem, vmem, vmem, vmem],
         out_specs=(hbm,) * 3,
         scratch_shapes=[pltpu.VMEM((rows, LANES), f32)] * 4
         + [pltpu.VMEM((4, EDGE, LANES), f32)] * 2
-        + [pltpu.SemaphoreType.DMA((3,))],
+        + [bounds, bounds, starts, pltpu.SemaphoreType.DMA((3,)), pltpu.SemaphoreType.DMA((3,))],
         compiler_params=pltpu.CompilerParams(vmem_limit_bytes=VMEM_LIMIT),
     )(old_bounds, new_bounds, seg_start, state, sums, left_rim, right_rim)
     return tuple(x.reshape(cap) for x in outs)

time: 27.6 us -> 19 us (0.69)
  local copies, waits for them, and re-layouts: 6.66 us -> 0 us
  Pallas kernels: 20 us -> 18.1 us
    unnamed x16 -> x0, local copies, waits for them, and re-layouts: 6.66 us -> none
    pallas_call x1, Pallas kernels: 4.76 us -> 2.77 us  [shards(): pl.pallas_call(functools.partial(update_kernel, axis), name='update', out...]
where the time goes in v2:
time: 19 us; the launch traced here: 18.8 us
  Pallas kernels  18.1 us (95%)
  between operations  0.65 us (3%)
    pallas_call x1, Pallas kernels, shards(): pl.pallas_call(functools.partial(exchange_kernel, axis, n), name='exchang...  10.7 us
    pallas_call x1, Pallas kernels, shards(): pl.pallas_call(functools.partial(place_kernel, axis), name='place', out_s...  4.7 us
    pallas_call x1, Pallas kernels, shards(): pl.pallas_call(functools.partial(update_kernel, axis), name='update', out...  2.77 us

profile of v2, /device:TPU:0, one launch (start us, length us, event | category | flops | bytes accessed | tf_op | source)
XLA Modules:
  0.0 18.8 jit_solution(16545211589772678876)
XLA Ops:
  0.6 2.8 %update.1 = (f32[4,1072,128]{2,1,0:T(8,128)S(1)}, f32[1,128]{1,0:T(1,128)S(1)}, f32[4,32,128]{2,1,0:T(8,128)S(1)}, f32[4,32,128]{2,1,0:T(8,128)S(1)}) custom-call(s32[33]{0:T(128)} %old_hbm.3, s32[64]{0:T(128)} %seg_hbm.3, f32[992,128]{1,0:T(8,128)} %bitcast.7, f32[992,128]{1,0:T(8,128)} %bitcast.8, f32[992,128]{1,0:T(8,128)} %bitcast.9, ...), custom_call_target="tpu_custom_call" | custom-call | tf_op jit(solution)/shard_map/update/pallas_call | solution.py:323
  3.4 10.7 %exchange.1 = (f32[1,128]{1,0:T(1,128)S(1)}, f32[4,32,128]{2,1,0:T(8,128)S(1)}, f32[4,32,128]{2,1,0:T(8,128)S(1)}) custom-call(f32[1,128]{1,0:T(1,128)S(1)} %get-tuple-element.14.part, f32[4,32,128]{2,1,0:T(8,128)S(1)} %get-tuple-element.15.tail, f32[4,32,128]{2,1,0:T(8,128)S(1)} %get-tuple-element.16.head), custom_call_target="tpu_custom_call" | custom-call | tf_op jit(solution)/shard_map/exchange/pallas_call | solution.py:340
  14.1 4.7 %place.1 = (f32[992,128]{1,0:T(8,128)}, f32[992,128]{1,0:T(8,128)}, f32[992,128]{1,0:T(8,128)}) custom-call(s32[33]{0:T(128)} %old_hbm.3, s32[33]{0:T(128)} %new_hbm.1, s32[64]{0:T(128)} %seg_hbm.3, f32[4,1072,128]{2,1,0:T(8,128)S(1)} %get-tuple-element.13.state, f32[1,128]{1,0:T(1,128)S(1)} %get-tuple-element.17.sums, ...), custom_call_target="tpu_custom_call" | custom-call | tf_op jit(solution)/shard_map/place/pallas_call | solution.py:358

commit v3 on v2

v3 whole, which is shorter than its diff:
```python
import functools

import jax
import jax.numpy as jnp
from jax import lax
from jax.experimental import pallas as pl
from jax.experimental.pallas import tpu as pltpu
from jax.sharding import PartitionSpec as P

MARGIN = 4096
LANES = 128
BLOCK = MARGIN // LANES
HALF = 64
HALF_BITS = 6
LANE_BITS = 7
PAD = BLOCK + 8
EDGE = 2 * PAD + BLOCK


BETA_ONE = 0.9
BETA_TWO = 0.999
CORR_ONE = 1.0 - 0.9**10
CORR_TWO = 1.0 - 0.999**10
DECAY = 0.01
LEARN = 0.1
EPSILON = 1e-06

MESH = pl.DeviceIdType.MESH
VMEM_LIMIT = 16 * 1024 * 1024


def lane_ids(rows=BLOCK):
    return lax.broadcasted_iota(jnp.int32, (rows, LANES), 1)


def flat_ids():
    return lax.broadcasted_iota(jnp.int32, (BLOCK, LANES), 0) * LANES + lane_ids()


def moved(first, second, lanes):
    picked = jnp.where(lane_ids() >= lanes, first, second)
    return pltpu.roll(picked, (LANES - lanes) & (LANES - 1), 1)


def overlapping(seg_ref, low, high):
    def step(s, carry):
        first, end = carry
        start = seg_ref[s]
        return (first + (start <= low).astype(jnp.int32), end + (start < high).astype(jnp.int32))

    first, end = lax.fori_loop(0, seg_ref.shape[0], step, (jnp.int32(-1), jnp.int32(0)), unroll=8)
    return first, end


def span_of(seg_ref, s, low, count):
    segs = seg_ref.shape[0]
    begin = jnp.maximum(seg_ref[s] - low, 0)
    after = seg_ref[jnp.minimum(s + 1, segs - 1)] - low
    finish = jnp.where(s + 1 < segs, jnp.minimum(after, count), count)
    return begin, finish


def fetched(tables, refs, sems):
    copies = [pltpu.make_async_copy(t, r, sems.at[i]) for i, (t, r) in enumerate(zip(tables, refs))]
    for copy in copies:
        copy.start()
    return copies


def step_kernel(
    axis, n, old_hbm, new_hbm, seg_hbm, w_hbm, m_hbm, v_hbm, g_hbm, placed, sums,
    state, m_buf, v_buf, g_buf, squares, member, begins, ends, part, tail, head, left_rim, right_rim,
    before, after, slots, old_ref, new_ref, seg_ref, sems, table_sems, send, receive, rim_send, rim_receive,
):
    rows = m_buf.shape[0]
    blocks = rows // BLOCK
    segs = seg_ref.shape[0]
    me = lax.axis_index(axis)
    right = lax.rem(me + 1, n)
    left = lax.rem(me + n - 1, n)
    tables = fetched((old_hbm, new_hbm, seg_hbm), (old_ref, new_ref, seg_ref), table_sems)
    step_blocks = -(-blocks // sems.shape[1])
    chunks = [(b, min(b + step_blocks, blocks)) for b in range(0, blocks, step_blocks)]
    copies = []
    for c, (b0, b1) in enumerate(chunks):
        window = pl.ds(b0 * BLOCK, (b1 - b0) * BLOCK)
        inside = state.at[0, pl.ds(PAD + b0 * BLOCK, (b1 - b0) * BLOCK)]
        group = [
            pltpu.make_async_copy(w_hbm.at[window], inside, sems.at[0, c]),
            pltpu.make_async_copy(m_hbm.at[window], m_buf.at[window], sems.at[1, c]),
            pltpu.make_async_copy(v_hbm.at[window], v_buf.at[window], sems.at[2, c]),
            pltpu.make_async_copy(g_hbm.at[window], g_buf.at[window], sems.at[3, c]),
        ]
        for copy in group:
            copy.start()
        copies.append(group)

    barrier = pltpu.get_barrier_semaphore()

    def greet(k, carry):
        pl.semaphore_signal(barrier, inc=1, device_id=(lax.rem(me + k, n),), device_id_type=MESH)
        return carry

    lax.fori_loop(1, n, greet, 0)

    for copy in tables:
        copy.wait()
    low = old_ref[me]
    count = old_ref[me + 1] - low
    new_low = new_ref[me]
    new_count = new_ref[me + 1] - new_low
    shift = new_low - low
    phase = (-low) & (HALF - 1)

    def bound(s, carry):
        value = (seg_ref[s] - low - phase) >> HALF_BITS
        begins[pl.ds(s, 1), :] = jnp.full((1, LANES), value, jnp.int32)
        following = (seg_ref[jnp.minimum(s + 1, segs - 1)] - low - phase) >> HALF_BITS
        following = jnp.where(s + 1 < segs, following, 4 * rows)
        ends[pl.ds(s, 1), :] = jnp.full((1, LANES), following, jnp.int32)
        return carry

    lax.fori_loop(0, segs, bound, 0, unroll=8)
    padded = member.shape[1]
    spot = lane_ids(segs)
    first_half = begins[...]
    past_half = ends[...]
    for group in range(3):
        for tile in range(padded // LANES):
            half = 2 * (spot + tile * LANES) - 1 + group
            mask = (half >= first_half) & (half < past_half)
            member[group * segs : (group + 1) * segs, tile * LANES : (tile + 1) * LANES] = jnp.where(
                mask, 1.0, 0.0
            ).astype(jnp.bfloat16)
    squares[rows:padded, :] = jnp.zeros((padded - rows, 4 * LANES), jnp.bfloat16)

    flat = flat_ids()

    def advance(b, carry):
        here = pl.multiple_of(b * BLOCK, BLOCK)
        there = pl.multiple_of(b * BLOCK + PAD, 8)
        gradient = g_buf[pl.ds(here, BLOCK), :].astype(jnp.float32)
        weight = state[0, pl.ds(there, BLOCK), :]
        moment = BETA_ONE * m_buf[pl.ds(here, BLOCK), :] + (1.0 - BETA_ONE) * gradient
        second = BETA_TWO * v_buf[pl.ds(here, BLOCK), :] + (1.0 - BETA_TWO) * gradient * gradient
        scaled = moment * (1.0 / CORR_ONE)
        update = scaled / (jnp.sqrt(second * (1.0 / CORR_TWO)) + EPSILON) + DECAY * weight
        state[1, pl.ds(there, BLOCK), :] = update
        state[2, pl.ds(there, BLOCK), :] = moment
        state[3, pl.ds(there, BLOCK), :] = second
        live = flat + b * MARGIN < count
        for i, value in enumerate((weight, update)):
            square = jnp.where(live, value * value, 0.0)
            coarse = square.astype(jnp.bfloat16)
            fine = (square - coarse.astype(jnp.float32)).astype(jnp.bfloat16)
            squares[pl.ds(here, BLOCK), i * LANES : (i + 1) * LANES] = coarse
            squares[pl.ds(here, BLOCK), (i + 2) * LANES : (i + 3) * LANES] = fine
        return carry

    for (b0, b1), group in zip(chunks, copies):
        for copy in group:
            copy.wait()
        lax.fori_loop(b0, b1, advance, 0)

    start = count - MARGIN
    start_row = start >> LANE_BITS
    start_lane = start & (LANES - 1)
    for a in range(4):
        head[a] = state[a, PAD : PAD + BLOCK, :]
        tail[a] = moved(
            state[a, pl.ds(PAD + start_row, BLOCK), :],
            state[a, pl.ds(PAD + start_row + 1, BLOCK), :],
            start_lane,
        )

    product = jnp.dot(member[...], squares[...], preferred_element_type=jnp.float32)
    product = product[:, : 2 * LANES] + product[:, 2 * LANES :]
    line = lax.broadcasted_iota(jnp.int32, (segs, LANES), 0)
    row = jnp.zeros((segs, LANES), jnp.float32)
    for i in range(2):
        columns = slice(i * LANES, (i + 1) * LANES)
        mixed = jnp.where(
            spot < phase,
            product[0:segs, columns],
            jnp.where(
                spot < phase + HALF, product[segs : 2 * segs, columns], product[2 * segs : 3 * segs, columns]
            ),
        )
        row = jnp.where(spot == line + i * segs, jnp.sum(mixed, axis=1, keepdims=True), row)
    part[...] = jnp.sum(row, axis=0, keepdims=True)
    slots[me] = part[...]
    pl.semaphore_wait(barrier, n - 1)

    def tell(k):
        return pltpu.make_async_remote_copy(
            src_ref=part,
            dst_ref=slots.at[me],
            send_sem=send.at[k],
            recv_sem=receive.at[k],
            device_id=(lax.rem(me + k, n),),
            device_id_type=MESH,
        )

    def hear(k):
        source = lax.rem(me + n - k, n)
        return pltpu.make_async_remote_copy(
            src_ref=part,
            dst_ref=slots.at[source],
            send_sem=send.at[k],
            recv_sem=receive.at[k],
            device_id=(source,),
            device_id_type=MESH,
        )

    onward = pltpu.make_async_remote_copy(
        src_ref=tail,
        dst_ref=left_rim,
        send_sem=rim_send.at[0],
        recv_sem=rim_receive.at[0],
        device_id=(right,),
        device_id_type=MESH,
    )
    back = pltpu.make_async_remote_copy(
        src_ref=head,
        dst_ref=right_rim,
        send_sem=rim_send.at[1],
        recv_sem=rim_receive.at[1],
        device_id=(left,),
        device_id_type=MESH,
    )

    def begin(k, carry):
        tell(k).start()
        return carry

    def finish(k, carry):
        tell(k).wait_send()
        hear(k).wait_recv()
        return carry

    lax.fori_loop(1, n, begin, 0)
    onward.start()
    back.start()

    top = shift >> LANE_BITS
    lanes = shift & (LANES - 1)

    def own(a, b):
        there = b * BLOCK + PAD + top
        return moved(state[a, pl.ds(there, BLOCK), :], state[a, pl.ds(there + 1, BLOCK), :], lanes)

    def inner(b, carry):
        here = pl.multiple_of(b * BLOCK, BLOCK)
        for a in range(4):
            placed[a, pl.ds(here, BLOCK), :] = own(a, b)
        return carry

    lax.fori_loop(1, blocks - 3, inner, 0)
    for a in range(4):
        before[a, BLOCK:EDGE, :] = state[a, PAD : PAD + EDGE - BLOCK, :]
    onward.wait()
    back.wait()
    for a in range(4):
        before[a, 0:BLOCK, :] = left_rim[a]
        after[a, PAD : PAD + BLOCK, :] = right_rim[a]
    for a in range(4):
        placed[a, 0:BLOCK, :] = moved(
            before[a, pl.ds(BLOCK + top, BLOCK), :], before[a, pl.ds(BLOCK + top + 1, BLOCK), :], lanes
        )

    for b in range(blocks - 3, blocks):
        offset = b * MARGIN + shift - count
        near = jnp.clip(offset >> LANE_BITS, -PAD, PAD - 7) + PAD
        side = offset & (LANES - 1)
        index = flat + b * MARGIN
        beyond = index + shift >= count
        live = index < new_count
        for a in range(4):
            rim = moved(after[a, pl.ds(near, BLOCK), :], after[a, pl.ds(near + 1, BLOCK), :], side)
            value = jnp.where(beyond, rim, own(a, b))
            placed[a, b * BLOCK : (b + 1) * BLOCK, :] = jnp.where(live, value, 0.0)

    lax.fori_loop(1, n, finish, 0)
    sums[...] = jnp.sum(slots[...], axis=0)


def apply_kernel(axis, new_hbm, seg_hbm, placed, sums, w_out, m_out, v_out, w_buf, new_ref, seg_ref, sems, table_sems):
    tables = fetched((new_hbm, seg_hbm), (new_ref, seg_ref), table_sems)
    m_copy = pltpu.make_async_copy(placed.at[2], m_out, sems.at[1])
    v_copy = pltpu.make_async_copy(placed.at[3], v_out, sems.at[2])
    m_copy.start()
    v_copy.start()
    rows = w_buf.shape[0]
    w_buf[...] = placed[0]
    segs = seg_ref.shape[0]
    total = sums[...]
    other = pltpu.roll(total, LANES - segs, 1)
    rate = LEARN * (jnp.sqrt(total) / (jnp.sqrt(other) + EPSILON))
    lane = lane_ids(1)
    flat = flat_ids()
    for copy in tables:
        copy.wait()
    me = lax.axis_index(axis)
    new_low = new_ref[me]
    new_high = new_ref[me + 1]
    new_count = new_high - new_low
    first, end = overlapping(seg_ref, new_low, new_high)

    def tensor(s, carry):
        begin, finish = span_of(seg_ref, s, new_low, new_count)
        factor = jnp.sum(jnp.where(lane == s, rate, 0.0), axis=1, keepdims=True)

        def apply(b, inner_carry):
            here = pl.ds(pl.multiple_of(b * BLOCK, BLOCK), BLOCK)
            index = flat + b * MARGIN
            inside = (index >= begin) & (index < finish)
            weight = w_buf[here, :]
            w_buf[here, :] = jnp.where(inside, weight - factor * placed[1, here, :], weight)
            return inner_carry

        return lax.fori_loop(begin // MARGIN, (finish + MARGIN - 1) // MARGIN, apply, carry)

    lax.fori_loop(first, end, tensor, 0)
    w_copy = pltpu.make_async_copy(w_buf, w_out, sems.at[0])
    w_copy.start()
    m_copy.wait()
    v_copy.wait()
    w_copy.wait()


def spec(space):
    return pl.BlockSpec(memory_space=space)


def shards(axis, n, params, first_moment, second_moment, grads, old_bounds, new_bounds, seg_start):
    cap = params.shape[0]
    rows = cap // LANES
    f32 = jnp.float32
    flat = [x.reshape(rows, LANES) for x in (params, first_moment, second_moment, grads)]
    old_bounds, new_bounds, seg_start, *flat = (
        pltpu.with_memory_space_constraint(x, pltpu.HBM) for x in (old_bounds, new_bounds, seg_start, *flat)
    )
    segs = seg_start.shape[0]
    padded = -(-rows // 256) * 256
    vmem, hbm = spec(pltpu.VMEM), spec(pltpu.HBM)
    bounds = pltpu.SMEM(old_bounds.shape, jnp.int32)
    starts = pltpu.SMEM(seg_start.shape, jnp.int32)
    rim = pltpu.VMEM((4, BLOCK, LANES), f32)
    dma = pltpu.SemaphoreType.DMA
    placed, sums = pl.pallas_call(
        functools.partial(step_kernel, axis, n),
        name="step",
        out_shape=(
            jax.ShapeDtypeStruct((4, rows, LANES), f32),
            jax.ShapeDtypeStruct((1, LANES), f32),
        ),
        in_specs=[hbm] * 7,
        out_specs=(vmem,) * 2,
        scratch_shapes=[
            pltpu.VMEM((4, rows + 2 * PAD, LANES), f32),
            pltpu.VMEM((rows, LANES), f32),
            pltpu.VMEM((rows, LANES), f32),
            pltpu.VMEM((rows, LANES), grads.dtype),
            pltpu.VMEM((padded, 4 * LANES), jnp.bfloat16),
            pltpu.VMEM((3 * segs, padded), jnp.bfloat16),
            pltpu.VMEM((segs, LANES), jnp.int32),
            pltpu.VMEM((segs, LANES), jnp.int32),
            pltpu.VMEM((1, LANES), f32),
            rim,
            rim,
            rim,
            rim,
            pltpu.VMEM((4, EDGE, LANES), f32),
            pltpu.VMEM((4, EDGE, LANES), f32),
            pltpu.VMEM((n, 1, LANES), f32),
            bounds,
            bounds,
            starts,
            dma((4, 4)),
            dma((3,)),
            dma((n,)),
            dma((n,)),
            dma((2,)),
            dma((2,)),
        ],
        compiler_params=pltpu.CompilerParams(
            collective_id=0, has_side_effects=True, vmem_limit_bytes=VMEM_LIMIT
        ),
    )(old_bounds, new_bounds, seg_start, *flat)
    whole = jax.ShapeDtypeStruct((rows, LANES), f32)
    outs = pl.pallas_call(
        functools.partial(apply_kernel, axis),
        name="apply",
        out_shape=(whole,) * 3,
        in_specs=[hbm, hbm, vmem, vmem],
        out_specs=(hbm,) * 3,
        scratch_shapes=[pltpu.VMEM((rows, LANES), f32), bounds, starts, dma((3,)), dma((2,))],
        compiler_params=pltpu.CompilerParams(vmem_limit_bytes=VMEM_LIMIT),
    )(new_bounds, seg_start, placed, sums)
    return tuple(x.reshape(cap) for x in outs)


def solution(mesh):
    (axis,) = mesh.axis_names
    n = mesh.shape[axis]
    placed = (P(axis), P(axis), P(axis), P(axis), P(), P(), P())
    return jax.shard_map(
        functools.partial(shards, axis, n),
        mesh=mesh,
        in_specs=placed,
        out_specs=(P(axis), P(axis), P(axis)),
        check_vma=False,
    )
```

time: 19 us -> 15.7 us (0.83)
  Pallas kernels: 18.1 us -> 14.9 us
    pallas_call x3 -> x2, Pallas kernels: 18.1 us -> 14.9 us  [the longest x1 12.8 us: shards(): pl.pallas_call(functools.partial(step_kernel, axis, n), name='step', out_...]
where the time goes in v3:
time: 15.7 us; the launch traced here: 15.6 us
  Pallas kernels  14.9 us (95%)
  between operations  0.64 us (4%)
    pallas_call x1, Pallas kernels, shards(): pl.pallas_call(functools.partial(step_kernel, axis, n), name='step', out_...  12.8 us
    pallas_call x1, Pallas kernels, shards(): pl.pallas_call(functools.partial(apply_kernel, axis), name='apply', out_s...  2.14 us

profile of v3, /device:TPU:0, one launch (start us, length us, event | category | flops | bytes accessed | tf_op | source)
XLA Modules:
  0.0 15.6 jit_solution(14285475510784878846)
XLA Ops:
  0.6 12.8 %step.1 = (f32[4,992,128]{2,1,0:T(8,128)S(1)}, f32[1,128]{1,0:T(1,128)S(1)}) custom-call(s32[33]{0:T(128)} %old_hbm.1, s32[33]{0:T(128)} %new_hbm.3, s32[64]{0:T(128)} %seg_hbm.3, f32[992,128]{1,0:T(8,128)} %bitcast.7, f32[992,128]{1,0:T(8,128)} %bitcast.8, f32[992,128]{1,0:T(8,128)} %bitcast.9, bf16[992,128]{1,0:T(8,128)(2,1)} %bitcast.10), custom_call_target="tpu_custom_call" | custom-call | tf_op jit(solution)/shard_map/step/pallas_call | solution.py:350
  13.4 2.1 %apply.1 = (f32[992,128]{1,0:T(8,128)}, f32[992,128]{1,0:T(8,128)}, f32[992,128]{1,0:T(8,128)}) custom-call(s32[33]{0:T(128)} %new_hbm.3, s32[64]{0:T(128)} %seg_hbm.3, f32[4,992,128]{2,1,0:T(8,128)S(1)} %get-tuple-element.8.placed, f32[1,128]{1,0:T(1,128)S(1)} %get-tuple-element.9.sums), custom_call_target="tpu_custom_call" | custom-call | tf_op jit(solution)/shard_map/apply/pallas_call | solution.py:391

commit v4 on v3

--- a/solution.py
+++ b/solution.py
@@ -42,24 +42,6 @@
     return pltpu.roll(picked, (LANES - lanes) & (LANES - 1), 1)
 
 
-def overlapping(seg_ref, low, high):
-    def step(s, carry):
-        first, end = carry
-        start = seg_ref[s]
-        return (first + (start <= low).astype(jnp.int32), end + (start < high).astype(jnp.int32))
-
-    first, end = lax.fori_loop(0, seg_ref.shape[0], step, (jnp.int32(-1), jnp.int32(0)), unroll=8)
-    return first, end
-
-
-def span_of(seg_ref, s, low, count):
-    segs = seg_ref.shape[0]
-    begin = jnp.maximum(seg_ref[s] - low, 0)
-    after = seg_ref[jnp.minimum(s + 1, segs - 1)] - low
-    finish = jnp.where(s + 1 < segs, jnp.minimum(after, count), count)
-    return begin, finish
-
-
 def fetched(tables, refs, sems):
     copies = [pltpu.make_async_copy(t, r, sems.at[i]) for i, (t, r) in enumerate(zip(tables, refs))]
     for copy in copies:
@@ -68,7 +50,7 @@
 
 
 def step_kernel(
-    axis, n, old_hbm, new_hbm, seg_hbm, w_hbm, m_hbm, v_hbm, g_hbm, placed, sums,
+    axis, n, old_hbm, new_hbm, seg_hbm, w_hbm, m_hbm, v_hbm, g_hbm, placed, sums, chosen,
     state, m_buf, v_buf, g_buf, squares, member, begins, ends, part, tail, head, left_rim, right_rim,
     before, after, slots, old_ref, new_ref, seg_ref, sems, table_sems, send, receive, rim_send, rim_receive,
 ):
@@ -112,15 +94,18 @@
     shift = new_low - low
     phase = (-low) & (HALF - 1)
 
-    def bound(s, carry):
-        value = (seg_ref[s] - low - phase) >> HALF_BITS
-        begins[pl.ds(s, 1), :] = jnp.full((1, LANES), value, jnp.int32)
-        following = (seg_ref[jnp.minimum(s + 1, segs - 1)] - low - phase) >> HALF_BITS
-        following = jnp.where(s + 1 < segs, following, 4 * rows)
-        ends[pl.ds(s, 1), :] = jnp.full((1, LANES), following, jnp.int32)
-        return carry
-
-    lax.fori_loop(0, segs, bound, 0, unroll=8)
+    def bound_all(origin, offset):
+        def bound(s, carry):
+            value = (seg_ref[s] - origin - offset) >> HALF_BITS
+            begins[pl.ds(s, 1), :] = jnp.full((1, LANES), value, jnp.int32)
+            following = (seg_ref[jnp.minimum(s + 1, segs - 1)] - origin - offset) >> HALF_BITS
+            following = jnp.where(s + 1 < segs, following, 4 * rows)
+            ends[pl.ds(s, 1), :] = jnp.full((1, LANES), following, jnp.int32)
+            return carry
+
+        lax.fori_loop(0, segs, bound, 0, unroll=8)
+
+    bound_all(low, phase)
     padded = member.shape[1]
     spot = lane_ids(segs)
     first_half = begins[...]
@@ -160,7 +145,7 @@
     for (b0, b1), group in zip(chunks, copies):
         for copy in group:
             copy.wait()
-        lax.fori_loop(b0, b1, advance, 0)
+        lax.fori_loop(b0, b1, advance, 0, unroll=2)
 
     start = count - MARGIN
     start_row = start >> LANE_BITS
@@ -188,27 +173,15 @@
         )
         row = jnp.where(spot == line + i * segs, jnp.sum(mixed, axis=1, keepdims=True), row)
     part[...] = jnp.sum(row, axis=0, keepdims=True)
-    slots[me] = part[...]
     pl.semaphore_wait(barrier, n - 1)
 
     def tell(k):
         return pltpu.make_async_remote_copy(
             src_ref=part,
             dst_ref=slots.at[me],
-            send_sem=send.at[k],
-            recv_sem=receive.at[k],
+            send_sem=send,
+            recv_sem=receive,
             device_id=(lax.rem(me + k, n),),
-            device_id_type=MESH,
-        )
-
-    def hear(k):
-        source = lax.rem(me + n - k, n)
-        return pltpu.make_async_remote_copy(
-            src_ref=part,
-            dst_ref=slots.at[source],
-            send_sem=send.at[k],
-            recv_sem=receive.at[k],
-            device_id=(source,),
             device_id_type=MESH,
         )
 
@@ -229,16 +202,9 @@
         device_id_type=MESH,
     )
 
-    def begin(k, carry):
+    for k in range(1, n):
         tell(k).start()
-        return carry
-
-    def finish(k, carry):
-        tell(k).wait_send()
-        hear(k).wait_recv()
-        return carry
-
-    lax.fori_loop(1, n, begin, 0)
+    pltpu.make_async_copy(part, slots.at[me], receive).start()
     onward.start()
     back.start()
 
@@ -255,7 +221,7 @@
             placed[a, pl.ds(here, BLOCK), :] = own(a, b)
         return carry
 
-    lax.fori_loop(1, blocks - 3, inner, 0)
+    lax.fori_loop(1, blocks - 3, inner, 0, unroll=3)
     for a in range(4):
         before[a, BLOCK:EDGE, :] = state[a, PAD : PAD + EDGE - BLOCK, :]
     onward.wait()
@@ -280,52 +246,75 @@
             value = jnp.where(beyond, rim, own(a, b))
             placed[a, b * BLOCK : (b + 1) * BLOCK, :] = jnp.where(live, value, 0.0)
 
-    lax.fori_loop(1, n, finish, 0)
-    sums[...] = jnp.sum(slots[...], axis=0)
-
-
-def apply_kernel(axis, new_hbm, seg_hbm, placed, sums, w_out, m_out, v_out, w_buf, new_ref, seg_ref, sems, table_sems):
-    tables = fetched((new_hbm, seg_hbm), (new_ref, seg_ref), table_sems)
-    m_copy = pltpu.make_async_copy(placed.at[2], m_out, sems.at[1])
-    v_copy = pltpu.make_async_copy(placed.at[3], v_out, sems.at[2])
+    new_phase = (-new_low) & (HALF - 1)
+    bound_all(new_low, new_phase)
+    on_lane = (spot & (segs - 1)) == line
+    lows = jnp.sum(jnp.where(on_lane, begins[...], 0), axis=0, keepdims=True)
+    highs = jnp.sum(jnp.where(on_lane, ends[...], 0), axis=0, keepdims=True)
+    block_row = lax.broadcasted_iota(jnp.int32, (BLOCK, LANES), 0)
+    lane_group = lane_ids() >> HALF_BITS
+
+    def choose(b, carry):
+        here = pl.multiple_of(b * BLOCK, BLOCK)
+        for tile in range(2):
+            half = 2 * (block_row + b * BLOCK) - 1 + 2 * tile + lane_group
+            mask = (half >= lows) & (half < highs)
+            chosen[pl.ds(here, BLOCK), tile * LANES : (tile + 1) * LANES] = jnp.where(mask, 1.0, 0.0).astype(
+                jnp.bfloat16
+            )
+        return carry
+
+    lax.fori_loop(0, blocks, choose, 0, unroll=2)
+    sums[1:2, :] = jnp.full((1, LANES), new_phase, jnp.int32).astype(jnp.float32)
+
+    pltpu.make_async_copy(slots, slots, receive).wait()
+    sums[0:1, :] = jnp.sum(slots[...], axis=0)
+    others = slots.at[pl.ds(0, n - 1)]
+    pltpu.make_async_copy(others, others, send).wait()
+
+
+def apply_kernel(segs, placed, sums, chosen, w_out, m_out, v_out, w_buf, sems):
+    m_copy = pltpu.make_async_copy(placed.at[2], m_out, sems.at[0])
+    v_copy = pltpu.make_async_copy(placed.at[3], v_out, sems.at[1])
     m_copy.start()
     v_copy.start()
     rows = w_buf.shape[0]
-    w_buf[...] = placed[0]
-    segs = seg_ref.shape[0]
-    total = sums[...]
+    total = sums[0:1, :]
+    phase = sums[1:2, :]
     other = pltpu.roll(total, LANES - segs, 1)
     rate = LEARN * (jnp.sqrt(total) / (jnp.sqrt(other) + EPSILON))
-    lane = lane_ids(1)
-    flat = flat_ids()
-    for copy in tables:
+    spot = lane_ids(segs)
+    line = lax.broadcasted_iota(jnp.int32, (segs, LANES), 0)
+    column = jnp.sum(jnp.where(spot == line, rate, 0.0), axis=1, keepdims=True)
+    place = spot.astype(jnp.float32)
+    early = place < phase
+    late = place >= phase + HALF
+    nothing = jnp.zeros((segs, LANES), jnp.float32)
+    rates = jnp.concatenate(
+        [
+            jnp.where(early, column, 0.0),
+            jnp.where(early | late, 0.0, column),
+            jnp.where(late, column, 0.0),
+            nothing,
+        ],
+        axis=0,
+    )
+    coarse = rates.astype(jnp.bfloat16)
+    fine = (rates - coarse.astype(jnp.float32)).astype(jnp.bfloat16)
+    table = jnp.concatenate([coarse, fine], axis=1)
+    step = 256
+    copies = []
+    for c, r0 in enumerate(range(0, rows, step)):
+        size = min(step, rows - r0)
+        product = jnp.dot(chosen[r0 : r0 + size, :], table, preferred_element_type=jnp.float32)
+        factor = product[:, :LANES] + product[:, LANES:]
+        w_buf[r0 : r0 + size, :] = placed[0, r0 : r0 + size, :] - factor * placed[1, r0 : r0 + size, :]
+        window = pl.ds(r0, size)
+        copy = pltpu.make_async_copy(w_buf.at[window], w_out.at[window], sems.at[2 + c])
+        copy.start()
+        copies.append(copy)
+    for copy in (m_copy, v_copy, *copies):
         copy.wait()
-    me = lax.axis_index(axis)
-    new_low = new_ref[me]
-    new_high = new_ref[me + 1]
-    new_count = new_high - new_low
-    first, end = overlapping(seg_ref, new_low, new_high)
-
-    def tensor(s, carry):
-        begin, finish = span_of(seg_ref, s, new_low, new_count)
-        factor = jnp.sum(jnp.where(lane == s, rate, 0.0), axis=1, keepdims=True)
-
-        def apply(b, inner_carry):
-            here = pl.ds(pl.multiple_of(b * BLOCK, BLOCK), BLOCK)
-            index = flat + b * MARGIN
-            inside = (index >= begin) & (index < finish)
-            weight = w_buf[here, :]
-            w_buf[here, :] = jnp.where(inside, weight - factor * placed[1, here, :], weight)
-            return inner_carry
-
-        return lax.fori_loop(begin // MARGIN, (finish + MARGIN - 1) // MARGIN, apply, carry)
-
-    lax.fori_loop(first, end, tensor, 0)
-    w_copy = pltpu.make_async_copy(w_buf, w_out, sems.at[0])
-    w_copy.start()
-    m_copy.wait()
-    v_copy.wait()
-    w_copy.wait()
 
 
 def spec(space):
@@ -347,15 +336,16 @@
     starts = pltpu.SMEM(seg_start.shape, jnp.int32)
     rim = pltpu.VMEM((4, BLOCK, LANES), f32)
     dma = pltpu.SemaphoreType.DMA
-    placed, sums = pl.pallas_call(
+    placed, sums, chosen = pl.pallas_call(
         functools.partial(step_kernel, axis, n),
         name="step",
         out_shape=(
             jax.ShapeDtypeStruct((4, rows, LANES), f32),
-            jax.ShapeDtypeStruct((1, LANES), f32),
+            jax.ShapeDtypeStruct((2, LANES), f32),
+            jax.ShapeDtypeStruct((rows, 2 * LANES), jnp.bfloat16),
         ),
         in_specs=[hbm] * 7,
-        out_specs=(vmem,) * 2,
+        out_specs=(vmem,) * 3,
         scratch_shapes=[
             pltpu.VMEM((4, rows + 2 * PAD, LANES), f32),
             pltpu.VMEM((rows, LANES), f32),
@@ -376,10 +366,10 @@
             bounds,
             bounds,
             starts,
-            dma((4, 4)),
+            dma((4, 2)),
             dma((3,)),
-            dma((n,)),
-            dma((n,)),
+            dma,
+            dma,
             dma((2,)),
             dma((2,)),
         ],
@@ -389,14 +379,14 @@
     )(old_bounds, new_bounds, seg_start, *flat)
     whole = jax.ShapeDtypeStruct((rows, LANES), f32)
     outs = pl.pallas_call(
-        functools.partial(apply_kernel, axis),
+        functools.partial(apply_kernel, segs),
         name="apply",
         out_shape=(whole,) * 3,
-        in_specs=[hbm, hbm, vmem, vmem],
+        in_specs=[vmem] * 3,
         out_specs=(hbm,) * 3,
-        scratch_shapes=[pltpu.VMEM((rows, LANES), f32), bounds, starts, dma((3,)), dma((2,))],
+        scratch_shapes=[pltpu.VMEM((rows, LANES), f32), dma((2 + -(-rows // 256),))],
         compiler_params=pltpu.CompilerParams(vmem_limit_bytes=VMEM_LIMIT),
-    )(new_bounds, seg_start, placed, sums)
+    )(placed, sums, chosen)
     return tuple(x.reshape(cap) for x in outs)
 
 

time: 15.7 us -> 14.1 us (0.90)
  Pallas kernels: 14.9 us -> 13.3 us
    pallas_call x1, Pallas kernels: 2.14 us -> 1.24 us  [shards(): pl.pallas_call(functools.partial(apply_kernel, segs), name='apply', out_s...]
    pallas_call x1, Pallas kernels: 12.8 us -> 12.1 us  [shards(): pl.pallas_call(functools.partial(step_kernel, axis, n), name='step', out_...]
where the time goes in v4:
time: 14.1 us; the launch traced here: 14 us
  Pallas kernels  13.3 us (94%)
  between operations  0.64 us (5%)
    pallas_call x1, Pallas kernels, shards(): pl.pallas_call(functools.partial(step_kernel, axis, n), name='step', out_...  12.1 us
    pallas_call x1, Pallas kernels, shards(): pl.pallas_call(functools.partial(apply_kernel, segs), name='apply', out_s...  1.24 us

profile of v4, /device:TPU:0, one launch (start us, length us, event | category | flops | bytes accessed | tf_op | source)
XLA Modules:
  0.0 14.0 jit_solution(10435601412703746565)
XLA Ops:
  0.6 12.1 %step.1 = (f32[4,992,128]{2,1,0:T(8,128)S(1)}, f32[2,128]{1,0:T(2,128)S(1)}, bf16[992,256]{1,0:T(8,128)(2,1)S(1)}) custom-call(s32[33]{0:T(128)} %old_hbm.1, s32[33]{0:T(128)} %new_hbm.1, s32[64]{0:T(128)} %seg_hbm.1, f32[992,128]{1,0:T(8,128)} %bitcast.7, f32[992,128]{1,0:T(8,128)} %bitcast.8, f32[992,128]{1,0:T(8,128)} %bitcast.9, bf16[992,128]{1,0:T(8,128)(2,1)} %bitcast.10), custom_call_target="tpu_custom_call" | custom-call | tf_op jit(solution)/shard_map/step/pallas_call | solution.py:339
  12.7 1.2 %apply.1 = (f32[992,128]{1,0:T(8,128)}, f32[992,128]{1,0:T(8,128)}, f32[992,128]{1,0:T(8,128)}) custom-call(f32[4,992,128]{2,1,0:T(8,128)S(1)} %get-tuple-element.9.placed, f32[2,128]{1,0:T(2,128)S(1)} %get-tuple-element.10.sums, bf16[992,256]{1,0:T(8,128)(2,1)S(1)} %get-tuple-element.11.chosen), custom_call_target="tpu_custom_call" | custom-call | tf_op jit(solution)/shard_map/apply/pallas_call | solution.py:381
